TPU v7x, 32 devices: a whole 2x2x4 slice. The times are simulated.
32 devices in a mesh: ord: 8 (over z, y), blk: 4 (over x, core).
Axes of the slice: x: 2, y: 2, z: 4, core: 2. Of those that a mesh axis runs over, the one named last changes fastest.
Arguments:
- panel: bfloat16 [2880, 64, 2880], P('ord', 'blk'), as said below
- gauss: bfloat16 [2, 16, 2880, 2880], P(None, None, 'ord', 'blk'), may hold values from -2.3841858e-06 to 2.3841858e-06
- height: float32 [16], replicated, may hold values from 0.25 to 2.5
- order_map: int32 [2880], replicated, may hold values from 0 to 2879, as said below
- cycle_map: int32 [64], P('blk'), may hold values from 360 to 2519, as said below
Outputs:
- field: bfloat16 [5760, 3072], P('ord', 'blk')
Inputs may be any that keep to these rules, and one draw needn't show every extreme that they name: `order_map`: a permutation of 0 to 2879; the 360 slots of each index of ord hold consecutive orders in ascending order. `panel`: entries at degrees below the order of their slot are zero. `cycle_map`: distinct cycle numbers.
All inputs are finite; a program needn't handle non-finite values.
Results may differ from a plain program's by a relative error of at most 0.0068.
Values may be sent and summed in bfloat16 or wider, within the bound.
A program may use at most 256 MiB of HBM per device.

v0:
```python
import math
import jax
import jax.numpy as jnp
from jax import lax
from jax.sharding import PartitionSpec as P

ORDERS = 2880
TILE = 320
NLON = 5760


def cycle_angles(cycle_map):
    theta = math.pi * (cycle_map.astype(jnp.float32) + 0.5) / ORDERS
    return (jnp.cos(theta), jnp.sin(theta))


def legendre_tables(current, before, degree, orders, cosine, sine):
    deg = degree[None, None, :]
    order = orders[:, None, None]
    radial = (deg + 1.0) * current
    polar = (
        -(
            deg * cosine[None, :, None] * current
            - jnp.sqrt(jnp.maximum(deg * deg - order * order, 0.0)) * before
        )
        / sine[None, :, None]
    )
    azimuth = order * current / sine[None, :, None]
    return jnp.stack([radial, polar, azimuth], 2).astype(jnp.bfloat16)


def weighted(coef, degree, height):
    radial = jnp.exp(-(degree[None, :] + 2.0) * height[:, None] / ORDERS)
    return (coef.astype(jnp.float32) * radial[None, :, None, :]).astype(jnp.bfloat16)


def assemble(total, cycles, shells):
    count = total.shape[1]
    parts = total.reshape(2, count, cycles, 3, shells)
    g_part = parts[0]
    h_part = parts[1]
    cosine_part = jnp.concatenate([g_part[:, :, :2], -h_part[:, :, 2:]], 2)
    sine_part = jnp.concatenate([h_part[:, :, :2], g_part[:, :, 2:]], 2)
    return (
        jnp.stack([cosine_part, sine_part])
        .reshape(2, count, cycles * 3 * shells)
        .astype(jnp.bfloat16)
    )


def phase_angles(orders_int, position):
    phase = orders_int[:, None] * position[None, :] % NLON
    angle = phase.astype(jnp.float32) * (2.0 * math.pi / NLON)
    return (jnp.cos(angle), jnp.sin(angle))


def degree_sums(panel_src, edge, coef_src, orders, cosine, sine, height, base, first, last):
    count, cycles, _ = panel_src.shape
    shells = height.shape[0]

    def step(tile, total):
        offset = (tile * TILE - base).astype(jnp.int32)
        current = lax.dynamic_slice_in_dim(panel_src, offset, TILE, 2).astype(jnp.float32)
        earlier = lax.dynamic_slice_in_dim(panel_src, jnp.maximum(offset - 1, 0), TILE, 2).astype(
            jnp.float32
        )
        shifted = jnp.concatenate([edge[:, :, None].astype(jnp.float32), current[:, :, :-1]], 2)
        before = jnp.where(offset > 0, earlier, shifted)
        degree = (tile * TILE + jnp.arange(TILE)).astype(jnp.float32)
        tables = legendre_tables(current, before, degree, orders, cosine, sine).reshape(
            count, cycles * 3, TILE
        )
        weights = weighted(lax.dynamic_slice_in_dim(coef_src, offset, TILE, 3), degree, height)
        return total + jnp.einsum(
            "okl,gsol->goks", tables, weights, preferred_element_type=jnp.float32
        )

    init = jnp.zeros((2, count, cycles * 3, shells), jnp.float32)
    return lax.fori_loop(jnp.asarray(first, jnp.int32), jnp.asarray(last, jnp.int32), step, init)


def body(panel, gauss, height, order_map, cycle_map):
    count, cycles, degrees = panel.shape
    shells = height.shape[0]
    tiles = degrees // TILE
    cosine, sine = cycle_angles(cycle_map)
    coef = lax.all_gather(gauss, "blk", axis=3, tiled=True)
    here = lax.axis_index("ord")
    orders_int = lax.dynamic_slice_in_dim(order_map, here * count, count, 0)
    orders = orders_int.astype(jnp.float32)
    zero_edge = jnp.zeros((count, cycles), jnp.bfloat16)
    total = degree_sums(panel, zero_edge, coef, orders, cosine, sine, height, 0, 0, tiles)
    spectra = assemble(total, cycles, shells)
    spread = lax.all_to_all(spectra, "ord", split_axis=2, concat_axis=1, tiled=True)
    items = spread.shape[2]
    width = NLON // 8
    inner_cos, inner_sin = phase_angles(order_map, jnp.arange(width))
    start_cos, start_sin = phase_angles(order_map, jnp.arange(8) * width)

    def transform(block):
        block_cos = lax.dynamic_slice_in_dim(start_cos, block, 1, 1)
        block_sin = lax.dynamic_slice_in_dim(start_sin, block, 1, 1)
        table_cos = inner_cos * block_cos - inner_sin * block_sin
        table_sin = inner_sin * block_cos + inner_cos * block_sin
        tables = jnp.stack([table_cos, table_sin]).astype(jnp.bfloat16)
        return lax.dot_general(
            tables, spread, (((0, 1), (0, 1)), ((), ())), preferred_element_type=jnp.float32
        )

    field = lax.map(transform, jnp.arange(8)).reshape(NLON, items).astype(jnp.bfloat16)
    return lax.all_to_all(field, "ord", split_axis=0, concat_axis=1, tiled=True)


def solution(mesh):
    return jax.shard_map(
        body,
        mesh=mesh,
        in_specs=(P("ord", "blk", None), P(None, None, "ord", "blk"), P(), P(), P("blk")),
        out_specs=P("ord", "blk"),
        check_vma=False,
    )
```

profile of v0, /device:TPU:0, one launch (start us, length us, event | category | flops | bytes accessed | tf_op | source)
XLA Modules:
  0.0 1558.1 jit_solution(583133086494186010)
XLA Ops:
  6.5 24.1 %copy.29 = bf16[2,16,360,720]{2,1,0,3:T(8,128)(2,1)} copy(bf16[2,16,360,720]{3,2,1,0:T(8,128)(2,1)} %param.10) | data formatting | bytes 33177600 | tf_op args[1]
  31.5 49.6 %copy.31 = bf16[360,16,2880]{0,2,1:T(8,128)(2,1)} copy(bf16[360,16,2880]{2,1,0:T(8,128)(2,1)} %param.9) | data formatting | bytes 66355200
  81.1 367.9 %all-gather.2.cloned.1.call-done = bf16[2,16,360,2880]{2,1,0,3:T(8,128)(2,1)} async-done(((bf16[2,16,360,720]{2,1,0,3:T(8,128)(2,1)}), bf16[2,16,360,2880]{2,1,0,3:T(8,128)(2,1)}) %all-gather.2.cloned.1.call-update) | async-done | bytes 66355216 | tf_op jit(solution)/shard_map/all_gather | solution.py:87
  449.0 670.7 %while.25 = (s32[]{:T(128)}, f32[2,360,48,16]{2,3,0,1:T(8,128)}, bf16[2,16,360,2880]{2,1,0,3:T(8,128)(2,1)}, f32[16]{0:T(128)S(1)}, bf16[360,16,2880]{0,2,1:T(8,...) while((s32[]{:T(128)}, f32[2,360,48,16]{2,3,0,1:T(8,128)}, ...), condition=%wide.region_1.2_spmd.clone, body=%wide.region_0.1_spmd.clone.sunk | while | flops 405015680 | bytes 134444624 | solution.py:79
  471.0 18.0 %copy.44 = bf16[360,48,320,1]{2,1,3,0:T(8,128)(2,1)} copy(bf16[360,48,320,1]{0,2,1,3:T(8,128)(2,1)} %bitcast.76) | data formatting | bytes 22118400 | tf_op jit(solution)/shard_map/while/body/convert_element_type | solution.py:29
  543.1 18.0 %copy.44 = bf16[360,48,320,1]{2,1,3,0:T(8,128)(2,1)} copy(bf16[360,48,320,1]{0,2,1,3:T(8,128)(2,1)} %bitcast.76) | data formatting | bytes 22118400 | tf_op jit(solution)/shard_map/while/body/convert_element_type | solution.py:29
  617.9 18.0 %copy.44 = bf16[360,48,320,1]{2,1,3,0:T(8,128)(2,1)} copy(bf16[360,48,320,1]{0,2,1,3:T(8,128)(2,1)} %bitcast.76) | data formatting | bytes 22118400 | tf_op jit(solution)/shard_map/while/body/convert_element_type | solution.py:29
  692.7 18.0 %copy.44 = bf16[360,48,320,1]{2,1,3,0:T(8,128)(2,1)} copy(bf16[360,48,320,1]{0,2,1,3:T(8,128)(2,1)} %bitcast.76) | data formatting | bytes 22118400 | tf_op jit(solution)/shard_map/while/body/convert_element_type | solution.py:29
  767.5 18.0 %copy.44 = bf16[360,48,320,1]{2,1,3,0:T(8,128)(2,1)} copy(bf16[360,48,320,1]{0,2,1,3:T(8,128)(2,1)} %bitcast.76) | data formatting | bytes 22118400 | tf_op jit(solution)/shard_map/while/body/convert_element_type | solution.py:29
  842.4 18.0 %copy.44 = bf16[360,48,320,1]{2,1,3,0:T(8,128)(2,1)} copy(bf16[360,48,320,1]{0,2,1,3:T(8,128)(2,1)} %bitcast.76) | data formatting | bytes 22118400 | tf_op jit(solution)/shard_map/while/body/convert_element_type | solution.py:29
  917.2 18.0 %copy.44 = bf16[360,48,320,1]{2,1,3,0:T(8,128)(2,1)} copy(bf16[360,48,320,1]{0,2,1,3:T(8,128)(2,1)} %bitcast.76) | data formatting | bytes 22118400 | tf_op jit(solution)/shard_map/while/body/convert_element_type | solution.py:29
  992.1 18.0 %copy.44 = bf16[360,48,320,1]{2,1,3,0:T(8,128)(2,1)} copy(bf16[360,48,320,1]{0,2,1,3:T(8,128)(2,1)} %bitcast.76) | data formatting | bytes 22118400 | tf_op jit(solution)/shard_map/while/body/convert_element_type | solution.py:29
  1066.9 18.0 %copy.44 = bf16[360,48,320,1]{2,1,3,0:T(8,128)(2,1)} copy(bf16[360,48,320,1]{0,2,1,3:T(8,128)(2,1)} %bitcast.76) | data formatting | bytes 22118400 | tf_op jit(solution)/shard_map/while/body/convert_element_type | solution.py:29
  1135.3 27.8 %all-to-all-done = bf16[2,360,768]{1,0,2:T(2,128)(2,1)S(1)} async-done(((bf16[2,360,768]{1,0,2:T(2,128)(2,1)}), bf16[2,360,768]{1,0,2:T(2,128)(2,1)S(1)}, u32[]{:S(2)}, u32[]{:S(2)}) %all-to-all-start) | async-done | bytes 1105952 | tf_op jit(solution)/shard_map/all_to_all | solution.py:94
  1164.7 352.7 %while.26 = (s32[]{:T(128)}, bf16[8,720,96]{1,2,0:T(8,128)(2,1)S(1)}, s32[8]{0:T(128)S(1)}, f32[2880,8]{0,1:T(8,128)}, f32[2880,8]{0,1:T(8,128)}, /*index=5*/bf1...) while((s32[]{:T(128)}, ...), condition=%wide.region_3.4_spmd.clone.clone, body=%wide.region_2.3_spmd.clone.clone.sunk | while | flops 835660800 | bytes 18279324 | solution.py:110
  1168.2 37.8 %fusion.58 = (bf16[1,2880,720]{1,2,0:T(8,128)(2,1)S(1)}, bf16[1,2880,720]{1,2,0:T(8,128)(2,1)S(1)}) fusion(s32[2880]{0:T(1024)S(1)} %get-tuple-element.493, f32[2880]{0:T(1024)S(1)} %get-tuple-element.418, f32[2880]{0:T(1024)S(1)} %get-tuple-element.419), kind=kLoop, calls=%fused_computation.32.clone.1 | loop fusion | flops 35251200 | bytes 8328960 | tf_op jit(solution)/shard_map/convert
  1212.3 37.8 %fusion.58 = (bf16[1,2880,720]{1,2,0:T(8,128)(2,1)S(1)}, bf16[1,2880,720]{1,2,0:T(8,128)(2,1)S(1)}) fusion(s32[2880]{0:T(1024)S(1)} %get-tuple-element.493, f32[2880]{0:T(1024)S(1)} %get-tuple-element.418, f32[2880]{0:T(1024)S(1)} %get-tuple-element.419), kind=kLoop, calls=%fused_computation.32.clone.1 | loop fusion | flops 35251200 | bytes 8328960 | tf_op jit(solution)/shard_map/convert
  1256.4 37.8 %fusion.58 = (bf16[1,2880,720]{1,2,0:T(8,128)(2,1)S(1)}, bf16[1,2880,720]{1,2,0:T(8,128)(2,1)S(1)}) fusion(s32[2880]{0:T(1024)S(1)} %get-tuple-element.493, f32[2880]{0:T(1024)S(1)} %get-tuple-element.418, f32[2880]{0:T(1024)S(1)} %get-tuple-element.419), kind=kLoop, calls=%fused_computation.32.clone.1 | loop fusion | flops 35251200 | bytes 8328960 | tf_op jit(solution)/shard_map/convert
  1300.5 37.8 %fusion.58 = (bf16[1,2880,720]{1,2,0:T(8,128)(2,1)S(1)}, bf16[1,2880,720]{1,2,0:T(8,128)(2,1)S(1)}) fusion(s32[2880]{0:T(1024)S(1)} %get-tuple-element.493, f32[2880]{0:T(1024)S(1)} %get-tuple-element.418, f32[2880]{0:T(1024)S(1)} %get-tuple-element.419), kind=kLoop, calls=%fused_computation.32.clone.1 | loop fusion | flops 35251200 | bytes 8328960 | tf_op jit(solution)/shard_map/convert
  1344.6 37.8 %fusion.58 = (bf16[1,2880,720]{1,2,0:T(8,128)(2,1)S(1)}, bf16[1,2880,720]{1,2,0:T(8,128)(2,1)S(1)}) fusion(s32[2880]{0:T(1024)S(1)} %get-tuple-element.493, f32[2880]{0:T(1024)S(1)} %get-tuple-element.418, f32[2880]{0:T(1024)S(1)} %get-tuple-element.419), kind=kLoop, calls=%fused_computation.32.clone.1 | loop fusion | flops 35251200 | bytes 8328960 | tf_op jit(solution)/shard_map/convert
  1388.7 37.8 %fusion.58 = (bf16[1,2880,720]{1,2,0:T(8,128)(2,1)S(1)}, bf16[1,2880,720]{1,2,0:T(8,128)(2,1)S(1)}) fusion(s32[2880]{0:T(1024)S(1)} %get-tuple-element.493, f32[2880]{0:T(1024)S(1)} %get-tuple-element.418, f32[2880]{0:T(1024)S(1)} %get-tuple-element.419), kind=kLoop, calls=%fused_computation.32.clone.1 | loop fusion | flops 35251200 | bytes 8328960 | tf_op jit(solution)/shard_map/convert
  1432.8 37.8 %fusion.58 = (bf16[1,2880,720]{1,2,0:T(8,128)(2,1)S(1)}, bf16[1,2880,720]{1,2,0:T(8,128)(2,1)S(1)}) fusion(s32[2880]{0:T(1024)S(1)} %get-tuple-element.493, f32[2880]{0:T(1024)S(1)} %get-tuple-element.418, f32[2880]{0:T(1024)S(1)} %get-tuple-element.419), kind=kLoop, calls=%fused_computation.32.clone.1 | loop fusion | flops 35251200 | bytes 8328960 | tf_op jit(solution)/shard_map/convert
  1476.9 37.8 %fusion.58 = (bf16[1,2880,720]{1,2,0:T(8,128)(2,1)S(1)}, bf16[1,2880,720]{1,2,0:T(8,128)(2,1)S(1)}) fusion(s32[2880]{0:T(1024)S(1)} %get-tuple-element.493, f32[2880]{0:T(1024)S(1)} %get-tuple-element.418, f32[2880]{0:T(1024)S(1)} %get-tuple-element.419), kind=kLoop, calls=%fused_computation.32.clone.1 | loop fusion | flops 35251200 | bytes 8328960 | tf_op jit(solution)/shard_map/convert
  1517.4 32.5 %all_to_all.34 = bf16[8,720,96]{1,2,0:T(8,128)(2,1)S(1)} all-to-all(bf16[8,720,96]{1,2,0:T(8,128)(2,1)S(1)} %get-tuple-element.155), channel_id=1, replica_groups=mesh['ord'=8,'blk'=4] {'ord'}, dimensions={0} | all-to-all | bytes 2211840 | tf_op jit(solution)/shard_map/all_to_all | solution.py:111
  (164 shorter events, 562.3 us)
Async XLA Ops:
  6.5 442.5 %all-gather.2.cloned.1.call-start = ((), (), s32[]{:S(2)}) async-start(), calls=%async_computation.2 | async-start | bytes 88473600 | tf_op jit(solution)/shard_map/all_gather | solution.py:87
  31.4 49.6 %copy-start.2 = (s32[16]{0:T(128)S(1)}, s32[16]{0:T(128)}, u32[]{:S(2)}) copy-start(s32[16]{0:T(128)} %param.13) | copy-start | bytes 196
  31.5 417.6 %copy-start.1 = (f32[16]{0:T(128)S(1)}, f32[16]{0:T(128)}, u32[]{:S(2)}) copy-start(f32[16]{0:T(128)} %param.11) | copy-start | bytes 196
  1125.6 8.6 copy-start
  1128.6 34.5 %all-to-all-start = ((bf16[2,360,768]{1,0,2:T(2,128)(2,1)}), bf16[2,360,768]{1,0,2:T(2,128)(2,1)S(1)}, u32[]{:S(2)}, u32[]{:S(2)}) async-start(bf16[2,360,768]{1,0,2:T(2,128)(2,1)} %copy.34), calls=%async_computation | async-start | bytes 2359296 | tf_op jit(solution)/shard_map/all_to_all | solution.py:94
Sparse Core Ops, SparseCore 0:
  30.8 418.2 all-gather.1
where the time goes:
time: 1570 us; the launch traced here: 1560 us
  other arithmetic  503 us (32%)
  local copies, waits for them, and re-layouts  446 us (28%)
  waiting for transfers between devices  396 us (25%)
  matrix products  146 us (9%)
  blocking collectives  32.5 us (2%)
    all_gather x1, waiting for transfers between devices, body(): coef = lax.all_gather(gauss, 'blk', axis=3, tiled=True)  368 us
    another operation x9, other arithmetic  303 us
    dynamic_slice x18, local copies, waits for them, and re-layouts, step(): lax.dynamic_slice_in_dim(coef_src, offset, TILE, 3)  186 us
    convert_element_type x9, local copies, waits for them, and re-layouts, legendre_tables(): return jnp.stack([radial, polar, azimuth], 2).astype(jnp.bfloat16)  162 us
    another operation x18, other arithmetic, legendre_tables(): return jnp.stack([radial, polar, azimuth], 2).astype(jnp.bfloat16)  141 us
    dot_general x9, matrix products, step(): jnp.einsum('okl,gsol->goks', tables, weights, preferred_element_type=jnp....  124 us
    unnamed x8, local copies, waits for them, and re-layouts  73.7 us
    convert_element_type x9, other arithmetic, step(): lax.dynamic_slice_in_dim(panel_src, offset, TILE, 2).astype(jnp.float32)  54.1 us
  transfers between devices with their start and end apart: 2, of which 2 were waited for; matrix products, arithmetic and copies ran while one was open for 3% of the time, Pallas kernels for 0%

commit v1 on v0

--- a/solution.py
+++ b/solution.py
@@ -84,7 +84,7 @@
     shells = height.shape[0]
     tiles = degrees // TILE
     cosine, sine = cycle_angles(cycle_map)
-    coef = lax.all_gather(gauss, "blk", axis=3, tiled=True)
+    coef = jnp.concatenate(lax.all_gather(gauss, "blk"), axis=3)
     here = lax.axis_index("ord")
     orders_int = lax.dynamic_slice_in_dim(order_map, here * count, count, 0)
     orders = orders_int.astype(jnp.float32)

time: 1570 us -> 1540 us (0.981)
  other arithmetic: 503 us -> 457 us
    reshape x0 -> x2, local copies, waits for them, and re-layouts: none -> 215 us  [body(): coef = jnp.concatenate(lax.all_gather(gauss, 'blk'), axis=3)]
    dynamic_slice x18 -> x0, local copies, waits for them, and re-layouts: 186 us -> none  [step(): lax.dynamic_slice_in_dim(coef_src, offset, TILE, 3)]
    convert_element_type x9, other arithmetic: 54.1 us -> 26.4 us  [step(): lax.dynamic_slice_in_dim(panel_src, offset, TILE, 2).astype(jnp.float32)]
    unnamed x8 -> x7, local copies, waits for them, and re-layouts: 73.7 us -> 49.9 us
    another operation x18, other arithmetic: 141 us -> 122 us  [legendre_tables(): return jnp.stack([radial, polar, azimuth], 2).astype(jnp.bfloat16)]
where the time goes in v1:
time: 1540 us; the launch traced here: 1530 us
  other arithmetic  457 us (30%)
  local copies, waits for them, and re-layouts  450 us (29%)
  waiting for transfers between devices  398 us (26%)
  matrix products  154 us (10%)
  blocking collectives  32.5 us (2%)
  loops' own time  15.7 us (1%)
    all_gather x1, waiting for transfers between devices, body(): coef = jnp.concatenate(lax.all_gather(gauss, 'blk'), axis=3)  369 us
    another operation x9, other arithmetic  303 us
    reshape x2, local copies, waits for them, and re-layouts, body(): coef = jnp.concatenate(lax.all_gather(gauss, 'blk'), axis=3)  215 us
    convert_element_type x9, local copies, waits for them, and re-layouts, legendre_tables(): return jnp.stack([radial, polar, azimuth], 2).astype(jnp.bfloat16)  161 us
    dot_general x9, matrix products, step(): jnp.einsum('okl,gsol->goks', tables, weights, preferred_element_type=jnp....  132 us
    another operation x18, other arithmetic, legendre_tables(): return jnp.stack([radial, polar, azimuth], 2).astype(jnp.bfloat16)  122 us
    unnamed x7, local copies, waits for them, and re-layouts  49.9 us
    all_to_all x1, blocking collectives, body(): return lax.all_to_all(field, 'ord', split_axis=0, concat_axis=1, tiled=True)  32.5 us
  transfers between devices with their start and end apart: 2, of which 2 were waited for; matrix products, arithmetic and copies ran while one was open for 3% of the time, Pallas kernels for 0%

profile of v1, /device:TPU:0, one launch (start us, length us, event | category | flops | bytes accessed | tf_op | source)
XLA Modules:
  0.0 1525.9 jit_solution(3254513842809596323)
XLA Ops:
  8.1 49.9 %copy.30 = bf16[360,16,2880]{0,2,1:T(8,128)(2,1)} copy(bf16[360,16,2880]{2,1,0:T(8,128)(2,1)} %param.9) | data formatting | bytes 66355200
  58.0 369.2 %all-gather.3.cloned.1.call-done = bf16[8,16,360,720]{3,2,1,0:T(8,128)(2,1)} async-done(((bf16[2,16,360,720]{3,2,1,0:T(8,128)(2,1)}), bf16[8,16,360,720]{3,2,1,0:T(8,128)(2,1)}) %all-gather.3.cloned.1.call-update) | async-done | bytes 66355216 | tf_op jit(solution)/shard_map/all_gather | solution.py:87
  427.2 88.9 %copy.29 = bf16[2,16,360,4,720]{4,3,1,0,2:T(4,128)(2,1)} copy(bf16[2,16,360,4,720]{4,2,1,0,3:T(8,128)(2,1)} %bitcast.1) | data formatting | bytes 132710400 | tf_op jit(solution)/shard_map/reshape | solution.py:87
  516.0 125.7 %reshape.313 = bf16[2,16,360,2880]{3,1,0,2:T(8,128)(2,1)} reshape(bf16[2,16,360,4,720]{4,3,1,0,2:T(4,128)(2,1)} %copy.29) | data formatting | bytes 132710400 | tf_op jit(solution)/shard_map/reshape | solution.py:87
  641.7 445.8 %while.25 = (s32[]{:T(128)}, f32[2,360,48,16]{2,3,0,1:T(8,128)}, bf16[2,16,360,2880]{3,1,0,2:T(8,128)(2,1)}, f32[16]{0:T(128)S(1)}, bf16[360,16,2880]{0,2,1:T(8,...) while((s32[]{:T(128)}, f32[2,360,48,16]{2,3,0,1:T(8,128)}, ...), condition=%wide.region_1.2_spmd.clone, body=%wide.region_0.1_spmd.clone.sunk | while | flops 405015680 | bytes 112326224 | solution.py:79
  658.8 17.9 %copy.41 = bf16[360,48,320,1]{2,1,3,0:T(8,128)(2,1)} copy(bf16[360,48,320,1]{0,2,1,3:T(8,128)(2,1)} %bitcast.81) | data formatting | bytes 22118400 | tf_op jit(solution)/shard_map/while/body/convert_element_type | solution.py:29
  706.0 17.9 %copy.41 = bf16[360,48,320,1]{2,1,3,0:T(8,128)(2,1)} copy(bf16[360,48,320,1]{0,2,1,3:T(8,128)(2,1)} %bitcast.81) | data formatting | bytes 22118400 | tf_op jit(solution)/shard_map/while/body/convert_element_type | solution.py:29
  755.9 17.9 %copy.41 = bf16[360,48,320,1]{2,1,3,0:T(8,128)(2,1)} copy(bf16[360,48,320,1]{0,2,1,3:T(8,128)(2,1)} %bitcast.81) | data formatting | bytes 22118400 | tf_op jit(solution)/shard_map/while/body/convert_element_type | solution.py:29
  805.7 17.9 %copy.41 = bf16[360,48,320,1]{2,1,3,0:T(8,128)(2,1)} copy(bf16[360,48,320,1]{0,2,1,3:T(8,128)(2,1)} %bitcast.81) | data formatting | bytes 22118400 | tf_op jit(solution)/shard_map/while/body/convert_element_type | solution.py:29
  855.7 17.9 %copy.41 = bf16[360,48,320,1]{2,1,3,0:T(8,128)(2,1)} copy(bf16[360,48,320,1]{0,2,1,3:T(8,128)(2,1)} %bitcast.81) | data formatting | bytes 22118400 | tf_op jit(solution)/shard_map/while/body/convert_element_type | solution.py:29
  905.6 17.9 %copy.41 = bf16[360,48,320,1]{2,1,3,0:T(8,128)(2,1)} copy(bf16[360,48,320,1]{0,2,1,3:T(8,128)(2,1)} %bitcast.81) | data formatting | bytes 22118400 | tf_op jit(solution)/shard_map/while/body/convert_element_type | solution.py:29
  955.5 17.9 %copy.41 = bf16[360,48,320,1]{2,1,3,0:T(8,128)(2,1)} copy(bf16[360,48,320,1]{0,2,1,3:T(8,128)(2,1)} %bitcast.81) | data formatting | bytes 22118400 | tf_op jit(solution)/shard_map/while/body/convert_element_type | solution.py:29
  1005.4 17.9 %copy.41 = bf16[360,48,320,1]{2,1,3,0:T(8,128)(2,1)} copy(bf16[360,48,320,1]{0,2,1,3:T(8,128)(2,1)} %bitcast.81) | data formatting | bytes 22118400 | tf_op jit(solution)/shard_map/while/body/convert_element_type | solution.py:29
  1103.0 27.8 %all-to-all-done = bf16[2,360,768]{1,0,2:T(2,128)(2,1)S(1)} async-done(((bf16[2,360,768]{1,0,2:T(2,128)(2,1)}), bf16[2,360,768]{1,0,2:T(2,128)(2,1)S(1)}, u32[]{:S(2)}, u32[]{:S(2)}) %all-to-all-start) | async-done | bytes 1105952 | tf_op jit(solution)/shard_map/all_to_all | solution.py:94
  1132.4 352.7 %while.26 = (s32[]{:T(128)}, bf16[8,720,96]{1,2,0:T(8,128)(2,1)S(1)}, s32[8]{0:T(128)S(1)}, f32[2880,8]{0,1:T(8,128)}, f32[2880,8]{0,1:T(8,128)}, /*index=5*/bf1...) while((s32[]{:T(128)}, ...), condition=%wide.region_3.4_spmd.clone.clone, body=%wide.region_2.3_spmd.clone.clone.sunk | while | flops 835660800 | bytes 18279332 | solution.py:110
  1135.9 37.8 %fusion.60 = (bf16[1,2880,720]{1,2,0:T(8,128)(2,1)S(1)}, bf16[1,2880,720]{1,2,0:T(8,128)(2,1)S(1)}) fusion(s32[2880]{0:T(1024)S(1)} %get-tuple-element.493, f32[2880]{0:T(1024)S(1)} %get-tuple-element.418, f32[2880]{0:T(1024)S(1)} %get-tuple-element.419), kind=kLoop, calls=%fused_computation.33.clone.1 | loop fusion | flops 35251200 | bytes 8328960 | tf_op jit(solution)/shard_map/convert
  1180.0 37.8 %fusion.60 = (bf16[1,2880,720]{1,2,0:T(8,128)(2,1)S(1)}, bf16[1,2880,720]{1,2,0:T(8,128)(2,1)S(1)}) fusion(s32[2880]{0:T(1024)S(1)} %get-tuple-element.493, f32[2880]{0:T(1024)S(1)} %get-tuple-element.418, f32[2880]{0:T(1024)S(1)} %get-tuple-element.419), kind=kLoop, calls=%fused_computation.33.clone.1 | loop fusion | flops 35251200 | bytes 8328960 | tf_op jit(solution)/shard_map/convert
  1224.1 37.8 %fusion.60 = (bf16[1,2880,720]{1,2,0:T(8,128)(2,1)S(1)}, bf16[1,2880,720]{1,2,0:T(8,128)(2,1)S(1)}) fusion(s32[2880]{0:T(1024)S(1)} %get-tuple-element.493, f32[2880]{0:T(1024)S(1)} %get-tuple-element.418, f32[2880]{0:T(1024)S(1)} %get-tuple-element.419), kind=kLoop, calls=%fused_computation.33.clone.1 | loop fusion | flops 35251200 | bytes 8328960 | tf_op jit(solution)/shard_map/convert
  1268.2 37.8 %fusion.60 = (bf16[1,2880,720]{1,2,0:T(8,128)(2,1)S(1)}, bf16[1,2880,720]{1,2,0:T(8,128)(2,1)S(1)}) fusion(s32[2880]{0:T(1024)S(1)} %get-tuple-element.493, f32[2880]{0:T(1024)S(1)} %get-tuple-element.418, f32[2880]{0:T(1024)S(1)} %get-tuple-element.419), kind=kLoop, calls=%fused_computation.33.clone.1 | loop fusion | flops 35251200 | bytes 8328960 | tf_op jit(solution)/shard_map/convert
  1312.3 37.8 %fusion.60 = (bf16[1,2880,720]{1,2,0:T(8,128)(2,1)S(1)}, bf16[1,2880,720]{1,2,0:T(8,128)(2,1)S(1)}) fusion(s32[2880]{0:T(1024)S(1)} %get-tuple-element.493, f32[2880]{0:T(1024)S(1)} %get-tuple-element.418, f32[2880]{0:T(1024)S(1)} %get-tuple-element.419), kind=kLoop, calls=%fused_computation.33.clone.1 | loop fusion | flops 35251200 | bytes 8328960 | tf_op jit(solution)/shard_map/convert
  1356.4 37.8 %fusion.60 = (bf16[1,2880,720]{1,2,0:T(8,128)(2,1)S(1)}, bf16[1,2880,720]{1,2,0:T(8,128)(2,1)S(1)}) fusion(s32[2880]{0:T(1024)S(1)} %get-tuple-element.493, f32[2880]{0:T(1024)S(1)} %get-tuple-element.418, f32[2880]{0:T(1024)S(1)} %get-tuple-element.419), kind=kLoop, calls=%fused_computation.33.clone.1 | loop fusion | flops 35251200 | bytes 8328960 | tf_op jit(solution)/shard_map/convert
  1400.5 37.8 %fusion.60 = (bf16[1,2880,720]{1,2,0:T(8,128)(2,1)S(1)}, bf16[1,2880,720]{1,2,0:T(8,128)(2,1)S(1)}) fusion(s32[2880]{0:T(1024)S(1)} %get-tuple-element.493, f32[2880]{0:T(1024)S(1)} %get-tuple-element.418, f32[2880]{0:T(1024)S(1)} %get-tuple-element.419), kind=kLoop, calls=%fused_computation.33.clone.1 | loop fusion | flops 35251200 | bytes 8328960 | tf_op jit(solution)/shard_map/convert
  1444.6 37.8 %fusion.60 = (bf16[1,2880,720]{1,2,0:T(8,128)(2,1)S(1)}, bf16[1,2880,720]{1,2,0:T(8,128)(2,1)S(1)}) fusion(s32[2880]{0:T(1024)S(1)} %get-tuple-element.493, f32[2880]{0:T(1024)S(1)} %get-tuple-element.418, f32[2880]{0:T(1024)S(1)} %get-tuple-element.419), kind=kLoop, calls=%fused_computation.33.clone.1 | loop fusion | flops 35251200 | bytes 8328960 | tf_op jit(solution)/shard_map/convert
  1485.1 32.5 %all_to_all.34 = bf16[8,720,96]{1,2,0:T(8,128)(2,1)S(1)} all-to-all(bf16[8,720,96]{1,2,0:T(8,128)(2,1)S(1)} %get-tuple-element.155), channel_id=1, replica_groups=mesh['ord'=8,'blk'=4] {'ord'}, dimensions={0} | all-to-all | bytes 2211840 | tf_op jit(solution)/shard_map/all_to_all | solution.py:111
  (147 shorter events, 356.6 us)
Async XLA Ops:
  6.5 420.6 %all-gather.3.cloned.1.call-start = ((), (), s32[]{:S(2)}) async-start(), calls=%async_computation.2 | async-start | bytes 88473600 | tf_op jit(solution)/shard_map/all_gather | solution.py:87
  8.1 49.9 %copy-start.2 = (s32[16]{0:T(128)S(1)}, s32[16]{0:T(128)}, u32[]{:S(2)}) copy-start(s32[16]{0:T(128)} %param.13) | copy-start | bytes 196
  516.0 125.7 %copy-start.1 = (f32[16]{0:T(128)S(1)}, f32[16]{0:T(128)}, u32[]{:S(2)}) copy-start(f32[16]{0:T(128)} %param.11) | copy-start | bytes 196
  1093.3 8.6 copy-start
  1096.3 34.5 %all-to-all-start = ((bf16[2,360,768]{1,0,2:T(2,128)(2,1)}), bf16[2,360,768]{1,0,2:T(2,128)(2,1)S(1)}, u32[]{:S(2)}, u32[]{:S(2)}) async-start(bf16[2,360,768]{1,0,2:T(2,128)(2,1)} %copy.33), calls=%async_computation | async-start | bytes 2359296 | tf_op jit(solution)/shard_map/all_to_all | solution.py:94
Sparse Core Ops, SparseCore 0:
  8.9 418.1 all-gather.2
